TPU v7x, 32 devices: a whole 2x2x4 slice. The times are simulated.
32 devices in a mesh: lat: 8 (over z, x), lev: 4 (over y, core).
Axes of the slice: x: 2, y: 2, z: 4, core: 2. Of those that a mesh axis runs over, the one named last changes fastest.
Arguments:
- grid: bfloat16 [640, 128, 4, 1280], P('lat', 'lev'), may hold values from -6 to 6
- legendre: bfloat16 [640, 640, 640], P('lat'), may hold values from -0.25 to 0.25
- vertical: bfloat16 [128, 128], P('lev'), may hold values from -0.5 to 0.5
- damping: bfloat16 [128], P('lev'), may hold values from 1 to 16
- lon_counts: int32 [640], replicated, may hold values from 160 to 1280
- wave_slots: int32 [640], replicated, may hold values from 0 to 639, as said below
Outputs:
- filtered_grid: bfloat16 [640, 128, 4, 1280], P('lat', 'lev')
Inputs may be any that keep to these rules, and one draw needn't show every extreme that they name: wave_slots is a permutation; slot g * 20 + r holds a wavenumber from r * 32 to (r + 1) * 32 - 1.
All inputs are finite; a program needn't handle non-finite values.
Results may differ from a plain program's by a relative error of at most 0.0074.
Values may be sent and summed in bfloat16 or wider, within the bound.
A program may use at most 512 MiB of HBM per device.

v0:
```python
import math
import jax
import jax.numpy as jnp
from jax import lax
from jax.sharding import PartitionSpec as P


def forward_build(wavenumbers, longitudes):
    points = jnp.arange(longitudes, dtype=jnp.int32)
    phase = (wavenumbers[:, None] * points[None, :] % longitudes).astype(jnp.float32) * (
        2.0 * math.pi / longitudes
    )
    scale = 1.0 / math.sqrt(longitudes)
    return jnp.stack([jnp.cos(phase) * scale, -jnp.sin(phase) * scale], axis=1).astype(jnp.bfloat16)


def inverse_build(wavenumbers, longitudes):
    points = jnp.arange(longitudes, dtype=jnp.int32)
    phase = (wavenumbers[:, None] * points[None, :] % longitudes).astype(jnp.float32) * (
        2.0 * math.pi / longitudes
    )
    scale = 1.0 / math.sqrt(longitudes)
    weight = jnp.where(wavenumbers == 0, 1.0, 2.0).astype(jnp.float32)[:, None]
    return jnp.stack(
        [jnp.cos(phase) * scale * weight, -jnp.sin(phase) * scale * weight], axis=1
    ).astype(jnp.bfloat16)


def damping_factor(degrees, damping):
    degree_values = jnp.arange(degrees).astype(jnp.float32)
    ratio = degree_values * (degree_values + 1.0) / float(degrees * (degrees - 1))
    return 1.0 / (1.0 + damping.astype(jnp.float32)[None, :] * (ratio * ratio)[:, None])


def legendre_forward(table, fourier, wavenumbers):
    degrees = table.shape[1]
    spectral = jnp.einsum("sna,srac->snrc", table, fourier, preferred_element_type=jnp.float32)
    live = (jnp.arange(degrees, dtype=jnp.int32)[None, :] >= wavenumbers[:, None]).astype(
        jnp.float32
    )
    return (spectral * live[:, :, None, None]).astype(jnp.bfloat16)


def legendre_inverse(table, mixed):
    banded = jnp.einsum("sna,snrc->srac", table, mixed, preferred_element_type=jnp.float32)
    return banded.astype(jnp.bfloat16)


def per_device(grid, legendre, vertical, damping, lon_counts, wave_slots):
    lat_rows, level_rows, fields, longitudes = grid.shape
    slot_count = wave_slots.shape[0]
    degrees = legendre.shape[1]
    forward_table = forward_build(wave_slots, longitudes)
    own_counts = lax.dynamic_slice_in_dim(lon_counts, lax.axis_index("lat") * lat_rows, lat_rows)
    fourier = jnp.einsum("mrx,alfx->mralf", forward_table, grid, preferred_element_type=jnp.float32)
    fourier = fourier.reshape(slot_count, 2, lat_rows, level_rows * fields)
    forward_kept = (2 * wave_slots[:, None] < own_counts[None, :]).astype(jnp.float32)
    fourier = (fourier * forward_kept[:, None, :, None]).astype(jnp.bfloat16)
    gathered = lax.all_to_all(fourier, "lat", split_axis=0, concat_axis=2, tiled=True)
    count = gathered.shape[0]
    own_waves = lax.dynamic_slice_in_dim(wave_slots, lax.axis_index("lat") * count, count)
    spectral = legendre_forward(legendre, gathered, own_waves)
    piece = lax.all_gather(spectral, "lev", axis=3, tiled=True)
    level_count = piece.shape[3] // fields
    block = piece.reshape(piece.shape[0], piece.shape[1], 2, level_count, fields)
    folded = jnp.einsum("snrkf,lk->snrlf", block, vertical, preferred_element_type=jnp.float32)
    own_part = spectral.reshape(count, degrees, 2, level_rows, fields).astype(jnp.float32)
    mixed = (own_part + folded) * damping_factor(degrees, damping)[None, :, None, :, None]
    mixed = mixed.astype(jnp.bfloat16).reshape(count, degrees, 2, level_rows * fields)
    banded = legendre_inverse(legendre, mixed)
    returned = lax.all_to_all(banded, "lat", split_axis=2, concat_axis=0, tiled=True)
    inverse_table = inverse_build(wave_slots, longitudes)
    back_kept = (2 * wave_slots[:, None] < own_counts[None, :]).astype(jnp.bfloat16)
    returned = returned * back_kept[:, None, :, None]
    filtered_grid = jnp.einsum(
        "mrac,mrx->acx", returned, inverse_table, preferred_element_type=jnp.float32
    )
    return filtered_grid.reshape(lat_rows, level_rows, fields, longitudes).astype(jnp.bfloat16)


def solution(mesh):
    return jax.shard_map(
        per_device,
        mesh=mesh,
        in_specs=(
            P("lat", "lev", None, None),
            P("lat", None, None),
            P("lev", None),
            P("lev"),
            P(),
            P(),
        ),
        out_specs=P("lat", "lev", None, None),
        check_vma=False,
    )
```

profile of v0, /device:TPU:0, one launch (start us, length us, event | category | flops | bytes accessed | tf_op | source)
XLA Modules:
  0.0 2570.0 jit_solution(2957762633101189925)
XLA Ops:
  6.5 0.0 copy-start
  6.5 0.7 broadcast_multiply_fusion
  7.2 0.7 select_multiply_fusion
  7.9 17.2 multiply_convert_fusion.3
  25.1 55.3 %fusion.9 = f32[640,2,80,32,4]{0,2,4,3,1:T(8,128)} fusion(bf16[80,32,4,1280]{3,2,1,0:T(4,128)(2,1)} %param.6, bf16[640,1,1280]{2,0,1:T(8,128)(2,1)S(1)} %get-tuple-element.9, bf16[640,1,1280]{2,0,1:T(8,128)(2,1)S(1)} %get-tuple-element.10), kind=kOutput, calls=%fused_computation.14 | convolution fusion | flops 33560985600 | bytes 81920000 | tf_op jit(solution)/shard_map/mrx,alfx->mralf/dot_general | solution.py:55
  80.4 58.4 %copy.27 = f32[640,2,80,128]{3,2,1,0:T(8,128)} copy(f32[640,2,80,128]{0,2,3,1:T(8,128)} %bitcast.69) | data formatting | bytes 104857600 | tf_op jit(solution)/shard_map/reshape | solution.py:56
  138.9 0.8 dynamic_slice.6
  139.6 0.8 compare_convert_fusion
  140.4 26.3 %multiply_convert_fusion.1 = bf16[640,2,80,128]{3,2,1,0:T(8,128)(2,1)} fusion(f32[640,2,80,128]{3,2,1,0:T(8,128)} %copy.27, f32[640,80]{1,0:T(8,128)S(1)} %get-tuple-element.8), kind=kLoop, calls=%fused_computation.11 | loop fusion | flops 26214400 | bytes 78848000 | tf_op jit(solution)/shard_map/convert_element_type | solution.py:58
  166.7 18.2 all-to-all-start
  184.9 0.0 all-gather.2.cloned.1.call-start
  185.0 0.8 dynamic_slice.7
  185.7 0.1 fusion.32
  185.8 565.9 %all-to-all-done = bf16[640,2,80,128]{3,2,1,0:T(8,128)(2,1)} async-done(((bf16[640,2,80,128]{3,2,1,0:T(8,128)(2,1)}), bf16[640,2,80,128]{3,2,1,0:T(8,128)(2,1)}, u32[]{:S(2)}, u32[]{:S(2)}) %all-to-all-start) | async-done | bytes 26214432 | tf_op jit(solution)/shard_map/all_to_all | solution.py:59
  751.8 21.8 copy.28
  773.6 42.9 %fusion.8 = bf16[80,640,2,128]{1,3,2,0:T(8,128)(2,1)} fusion(f32[80,640]{1,0:T(8,128)S(1)} %fusion.32, bf16[80,2,640,128]{3,2,1,0:T(8,128)(2,1)} %bitcast.71, bf16[80,640,640]{2,1,0:T(8,128)(2,1)} %param.7), kind=kOutput, calls=%fused_computation.12 | convolution fusion | flops 16803430400 | bytes 118169600 | tf_op jit(solution)/shard_map/sna,srac->snrc/dot_general | solution.py:37
  816.5 0.0 copy-start.5
  816.5 0.0 all-gather.2.cloned.1.call-update
  816.6 0.6 copy-done.5
  817.2 0.1 add_divide_fusion
  817.3 50.3 %reshape.290 = f32[80,640,2,32,4]{1,4,3,2,0:T(4,128)} reshape(bf16[80,640,2,128]{1,3,2,0:T(8,128)(2,1)} %fusion.8) | data formatting | bytes 78643200 | tf_op jit(solution)/shard_map/convert_element_type | solution.py:67
  867.6 557.3 %all-gather.2.cloned.1.call-done = bf16[80,640,2,512]{1,3,2,0:T(8,128)(2,1)} async-done(((bf16[80,640,2,128]{1,3,2,0:T(8,128)(2,1)}), bf16[80,640,2,512]{1,3,2,0:T(8,128)(2,1)}) %all-gather.2.cloned.1.call-update) | async-done | bytes 104857616 | tf_op jit(solution)/shard_map/all_gather | solution.py:63
  1424.9 168.4 %reshape.288 = bf16[80,640,2,128,4]{1,4,3,2,0:T(4,128)(2,1)} reshape(bf16[80,640,2,512]{1,3,2,0:T(8,128)(2,1)} %all-gather.2.cloned.1.call-done) | data formatting | bytes 209715200 | tf_op jit(solution)/shard_map/reshape | solution.py:65
  1593.3 0.0 copy-done
  1593.3 64.9 %fusion.7 = bf16[80,640,2,32,4]{1,3,4,2,0:T(8,128)(2,1)} fusion(f32[80,640,2,32,4]{1,4,3,2,0:T(4,128)} %reshape.290, f32[640,32]{0,1:T(8,128)S(1)} %add_divide_fusion, bf16[80,640,2,128,4]{1,4,3,2,0:T(4,128)(2,1)} %reshape.288, bf16[32,128]{1,0:T(8,128)(2,1)S(1)} %copy-done), kind=kOutput, calls=%fused_computation.9 | convolution fusion | flops 3394764800 | bytes 183590912 | tf_op jit(solution)/shard_map/snrkf,lk->snrlf/dot_general | solution.py:66
  1658.2 18.6 copy.32
  1676.8 54.9 %convert_bitcast_fusion = bf16[80,2,640,128]{2,3,1,0:T(8,128)(2,1)} fusion(bf16[80,640,640]{2,1,0:T(8,128)(2,1)} %param.7, bf16[80,640,2,128]{1,0,3,2:T(8,128)(2,1)} %bitcast.72), kind=kOutput, calls=%fused_computation.19 | convolution fusion | flops 16790323200 | bytes 117964800 | tf_op jit(solution)/shard_map/sna,snrc->srac/dot_general | solution.py:45
  1731.7 64.2 %copy.34 = bf16[80,2,640,128]{3,1,0,2:T(2,128)(2,1)} copy(bf16[80,2,640,128]{2,3,1,0:T(8,128)(2,1)} %convert_bitcast_fusion) | data formatting | bytes 52428800 | tf_op jit(solution)/shard_map/convert_element_type | solution.py:46
  1795.9 570.9 %all_to_all.36 = bf16[80,2,640,128]{3,1,0,2:T(2,128)(2,1)S(1)} all-to-all(bf16[80,2,640,128]{3,1,0,2:T(2,128)(2,1)} %copy.34), channel_id=1, replica_groups=mesh['lat'=8,'lev'=4] {'lat'}, dimensions={2} | all-to-all | bytes 52428800 | tf_op jit(solution)/shard_map/all_to_all | solution.py:71
  2366.9 12.7 copy.35
  2379.6 0.0 copy-start.4
  2379.6 21.3 copy.36
  2400.8 0.0 copy-done.4
  2400.8 18.0 bitcast_multiply_fusion
  2418.8 0.0 copy-start.2
  2418.8 0.0 copy-start.3
  2418.8 42.8 %copy.37 = bf16[80,128,640,2]{2,0,3,1:T(8,128)(2,1)} copy(bf16[80,128,640,2]{1,0,3,2:T(8,128)(2,1)} %bitcast.67) | data formatting | bytes 52428800 | tf_op jit(solution)/shard_map/mrac,mrx->acx/dot_general | solution.py:75
  2461.6 0.0 copy-done.2
  2461.6 0.0 copy-done.3
  2461.6 0.0 copy-start.1
  2461.7 71.1 %bitcast_convert_fusion = bf16[80,32,4,1280]{3,1,2,0:T(8,128)(2,1)} fusion(bf16[80,32,4,640,2]{3,0,4,2,1:T(8,128)(2,1)} %bitcast.70, bf16[640,1,1280]{2,0,1:T(8,128)(2,1)S(1)} %copy-done.3, bf16[640,1,1280]{2,0,1:T(8,128)(2,1)S(1)} %copy-done.2), kind=kOutput, calls=%fused_computation.6 | convolution fusion | flops 33569177600 | bytes 55705600 | tf_op jit(solution)/shard_map/mrac,mrx->acx/dot_general | solution.py:75
  2532.8 29.9 %copy.39 = bf16[80,32,4,1280]{3,2,1,0:T(4,128)(2,1)} copy(bf16[80,32,4,1280]{3,1,2,0:T(8,128)(2,1)} %bitcast_convert_fusion) | data formatting | bytes 52428800 | tf_op jit(solution)/shard_map/convert_element_type | solution.py:78
  2562.7 0.0 copy-done.1
  (2 shorter events, 0.0 us)
Async XLA Ops:
  6.5 1586.7 %copy-start = (bf16[32,128]{1,0:T(8,128)(2,1)S(1)}, bf16[32,128]{1,0:T(8,128)(2,1)}, u32[]{:S(2)}) copy-start(bf16[32,128]{1,0:T(8,128)(2,1)} %param.8) | copy-start | bytes 24580
  166.7 585.0 %all-to-all-start = ((bf16[640,2,80,128]{3,2,1,0:T(8,128)(2,1)}), bf16[640,2,80,128]{3,2,1,0:T(8,128)(2,1)}, u32[]{:S(2)}, u32[]{:S(2)}) async-start(bf16[640,2,80,128]{3,2,1,0:T(8,128)(2,1)} %multiply_convert_fusion.1), calls=%async_computation | async-start | bytes 52428800 | tf_op jit(solution)/shard_map/all_to_all | solution.py:59
  184.9 1240.0 %all-gather.2.cloned.1.call-start = ((), (), s32[]{:S(2)}) async-start(), calls=%async_computation.2 | async-start | bytes 131072000 | tf_op jit(solution)/shard_map/all_gather | solution.py:63
  816.5 0.7 copy-start.5
  2379.6 21.3 copy-start.4
  2418.8 42.8 %copy-start.2 = (bf16[640,1,1280]{2,0,1:T(8,128)(2,1)S(1)}, bf16[640,1,1280]{2,0,1:T(8,128)(2,1)}, u32[]{:S(2)}) copy-start(bf16[640,1,1280]{2,0,1:T(8,128)(2,1)} %get-tuple-element.5) | copy-start | bytes 4915204
  2418.8 42.9 %copy-start.3 = (bf16[640,1,1280]{2,0,1:T(8,128)(2,1)S(1)}, bf16[640,1,1280]{2,0,1:T(8,128)(2,1)}, u32[]{:S(2)}) copy-start(bf16[640,1,1280]{2,0,1:T(8,128)(2,1)} %get-tuple-element.6) | copy-start | bytes 4915204
  2461.6 101.1 %copy-start.1 = (bf16[32,128]{1,0:T(8,128)(2,1)S(1)}, bf16[32,128]{1,0:T(8,128)(2,1)}, u32[]{:S(2)}) copy-start(bf16[32,128]{1,0:T(8,128)(2,1)} %param.8) | copy-start | bytes 24580
Sparse Core Ops, SparseCore 0:
  816.7 608.1 all-gather.1
where the time goes:
time: 2590 us; the launch traced here: 2570 us
  waiting for transfers between devices  1120 us (43%)
  blocking collectives  571 us (22%)
  local copies, waits for them, and re-layouts  491 us (19%)
  matrix products  289 us (11%)
  other arithmetic  63.8 us (2%)
    all_to_all x1, blocking collectives, per_device(): lax.all_to_all(banded, 'lat', split_axis=2, concat_axis=0, tiled=True)  571 us
    all_to_all x1, waiting for transfers between devices, per_device(): lax.all_to_all(fourier, 'lat', split_axis=0, concat_axis=2, tiled=True)  566 us
    all_gather x1, waiting for transfers between devices, per_device(): piece = lax.all_gather(spectral, 'lev', axis=3, tiled=True)  557 us
    reshape x1, local copies, waits for them, and re-layouts, per_device(): piece.reshape(piece.shape[0], piece.shape[1], 2, level_count, fields)  168 us
    dot_general x1, matrix products, per_device(): jnp.einsum('mrac,mrx->acx', returned, inverse_table, preferred_element_ty...  71.1 us
    dot_general x1, matrix products, per_device(): jnp.einsum('snrkf,lk->snrlf', block, vertical, preferred_element_type=jnp...  64.9 us
    convert_element_type x1, local copies, waits for them, and re-layouts, legendre_inverse(): return banded.astype(jnp.bfloat16)  64.2 us
    reshape x1, local copies, waits for them, and re-layouts, per_device(): fourier = fourier.reshape(slot_count, 2, lat_rows, level_rows * fields)  58.4 us
  transfers between devices with their start and end apart: 2, of which 2 were waited for; matrix products, arithmetic and copies ran while one was open for 2% of the time, Pallas kernels for 0%

commit v1 on v0

--- a/solution.py
+++ b/solution.py
@@ -68,7 +68,9 @@
     mixed = (own_part + folded) * damping_factor(degrees, damping)[None, :, None, :, None]
     mixed = mixed.astype(jnp.bfloat16).reshape(count, degrees, 2, level_rows * fields)
     banded = legendre_inverse(legendre, mixed)
-    returned = lax.all_to_all(banded, "lat", split_axis=2, concat_axis=0, tiled=True)
+    pieces = jnp.split(banded, lax.axis_size("lat"), axis=2)
+    received = lax.all_to_all(jnp.stack(pieces), "lat", 0, 0)
+    returned = jnp.concatenate(received, axis=0)
     inverse_table = inverse_build(wave_slots, longitudes)
     back_kept = (2 * wave_slots[:, None] < own_counts[None, :]).astype(jnp.bfloat16)
     returned = returned * back_kept[:, None, :, None]

time: 2590 us -> 2590 us (level)
    convert_element_type x1 -> x0, local copies, waits for them, and re-layouts: 64.2 us -> none  [legendre_inverse(): return banded.astype(jnp.bfloat16)]
    unnamed x12 -> x19, local copies, waits for them, and re-layouts: 0.65 us -> 53.2 us
    another operation x0 -> x2, local copies, waits for them, and re-layouts: none -> 49.6 us  [per_device(): received = lax.all_to_all(jnp.stack(pieces), 'lat', 0, 0)]
    all_to_all x2 -> x0, local copies, waits for them, and re-layouts: 34 us -> none  [per_device(): lax.all_to_all(banded, 'lat', split_axis=2, concat_axis=0, tiled=True)]
where the time goes in v1:
time: 2590 us; the launch traced here: 2570 us
  waiting for transfers between devices  1120 us (43%)
  blocking collectives  575 us (22%)
  local copies, waits for them, and re-layouts  495 us (19%)
  matrix products  289 us (11%)
  other arithmetic  63.8 us (2%)
    all_to_all x1, blocking collectives, per_device(): received = lax.all_to_all(jnp.stack(pieces), 'lat', 0, 0)  575 us
    all_to_all x1, waiting for transfers between devices, per_device(): lax.all_to_all(fourier, 'lat', split_axis=0, concat_axis=2, tiled=True)  566 us
    all_gather x1, waiting for transfers between devices, per_device(): piece = lax.all_gather(spectral, 'lev', axis=3, tiled=True)  557 us
    reshape x1, local copies, waits for them, and re-layouts, per_device(): piece.reshape(piece.shape[0], piece.shape[1], 2, level_count, fields)  168 us
    dot_general x1, matrix products, per_device(): jnp.einsum('mrac,mrx->acx', returned, inverse_table, preferred_element_ty...  71 us
    dot_general x1, matrix products, per_device(): jnp.einsum('snrkf,lk->snrlf', block, vertical, preferred_element_type=jnp...  64.9 us
    reshape x1, local copies, waits for them, and re-layouts, per_device(): fourier = fourier.reshape(slot_count, 2, lat_rows, level_rows * fields)  58.4 us
    dot_general x1, matrix products, per_device(): jnp.einsum('mrx,alfx->mralf', forward_table, grid, preferred_element_type...  55.3 us
  transfers between devices with their start and end apart: 2, of which 2 were waited for; matrix products, arithmetic and copies ran while one was open for 2% of the time, Pallas kernels for 0%

profile of v1, /device:TPU:0, one launch (start us, length us, event | category | flops | bytes accessed | tf_op | source)
XLA Modules:
  0.0 2567.2 jit_solution(14363074901066134418)
XLA Ops:
  6.5 0.0 copy-start
  6.5 0.7 broadcast_multiply_fusion
  7.2 0.7 select_multiply_fusion
  7.9 17.2 multiply_convert_fusion.3
  25.1 55.3 %fusion.9 = f32[640,2,80,32,4]{0,2,4,3,1:T(8,128)} fusion(bf16[80,32,4,1280]{3,2,1,0:T(4,128)(2,1)} %param.6, bf16[640,1,1280]{2,0,1:T(8,128)(2,1)S(1)} %get-tuple-element.9, bf16[640,1,1280]{2,0,1:T(8,128)(2,1)S(1)} %get-tuple-element.10), kind=kOutput, calls=%fused_computation.14 | convolution fusion | flops 33560985600 | bytes 81920000 | tf_op jit(solution)/shard_map/mrx,alfx->mralf/dot_general | solution.py:55
  80.4 58.4 %copy.39 = f32[640,2,80,128]{3,2,1,0:T(8,128)} copy(f32[640,2,80,128]{0,2,3,1:T(8,128)} %bitcast.97) | data formatting | bytes 104857600 | tf_op jit(solution)/shard_map/reshape | solution.py:56
  138.9 0.8 dynamic_slice.6
  139.6 0.8 compare_convert_fusion
  140.4 26.3 %multiply_convert_fusion.1 = bf16[640,2,80,128]{3,2,1,0:T(8,128)(2,1)} fusion(f32[640,2,80,128]{3,2,1,0:T(8,128)} %copy.39, f32[640,80]{1,0:T(8,128)S(1)} %get-tuple-element.8), kind=kLoop, calls=%fused_computation.11 | loop fusion | flops 26214400 | bytes 78848000 | tf_op jit(solution)/shard_map/convert_element_type | solution.py:58
  166.7 7.3 all-to-all-start
  174.0 0.0 all-gather.2.cloned.1.call-start
  174.0 0.8 dynamic_slice.7
  174.8 0.1 fusion.40
  174.9 565.8 %all-to-all-done = bf16[640,2,80,128]{3,2,1,0:T(8,128)(2,1)} async-done(((bf16[640,2,80,128]{3,2,1,0:T(8,128)(2,1)}), bf16[640,2,80,128]{3,2,1,0:T(8,128)(2,1)}, u32[]{:S(2)}, u32[]{:S(2)}) %all-to-all-start) | async-done | bytes 26214432 | tf_op jit(solution)/shard_map/all_to_all | solution.py:59
  740.7 21.8 copy.40
  762.5 42.9 %fusion.8 = bf16[80,640,2,128]{1,3,2,0:T(8,128)(2,1)} fusion(f32[80,640]{1,0:T(8,128)S(1)} %fusion.40, bf16[80,2,640,128]{3,2,1,0:T(8,128)(2,1)} %bitcast.99, bf16[80,640,640]{2,1,0:T(8,128)(2,1)} %param.7), kind=kOutput, calls=%fused_computation.12 | convolution fusion | flops 16803430400 | bytes 118169600 | tf_op jit(solution)/shard_map/sna,srac->snrc/dot_general | solution.py:37
  805.4 0.0 copy-start.5
  805.4 0.0 all-gather.2.cloned.1.call-update
  805.5 0.6 copy-done.5
  806.1 0.1 add_divide_fusion
  806.2 50.3 %reshape.294 = f32[80,640,2,32,4]{1,4,3,2,0:T(4,128)} reshape(bf16[80,640,2,128]{1,3,2,0:T(8,128)(2,1)} %fusion.8) | data formatting | bytes 78643200 | tf_op jit(solution)/shard_map/convert_element_type | solution.py:67
  856.5 557.1 %all-gather.2.cloned.1.call-done = bf16[80,640,2,512]{1,3,2,0:T(8,128)(2,1)} async-done(((bf16[80,640,2,128]{1,3,2,0:T(8,128)(2,1)}), bf16[80,640,2,512]{1,3,2,0:T(8,128)(2,1)}) %all-gather.2.cloned.1.call-update) | async-done | bytes 104857616 | tf_op jit(solution)/shard_map/all_gather | solution.py:63
  1413.6 168.4 %reshape.291 = bf16[80,640,2,128,4]{1,4,3,2,0:T(4,128)(2,1)} reshape(bf16[80,640,2,512]{1,3,2,0:T(8,128)(2,1)} %all-gather.2.cloned.1.call-done) | data formatting | bytes 209715200 | tf_op jit(solution)/shard_map/reshape | solution.py:65
  1581.9 0.0 copy-done
  1581.9 64.9 %fusion.7 = bf16[80,640,2,32,4]{1,3,4,2,0:T(8,128)(2,1)} fusion(f32[80,640,2,32,4]{1,4,3,2,0:T(4,128)} %reshape.294, f32[640,32]{0,1:T(8,128)S(1)} %add_divide_fusion, bf16[80,640,2,128,4]{1,4,3,2,0:T(4,128)(2,1)} %reshape.291, bf16[32,128]{1,0:T(8,128)(2,1)S(1)} %copy-done), kind=kOutput, calls=%fused_computation.9 | convolution fusion | flops 3394764800 | bytes 183590912 | tf_op jit(solution)/shard_map/snrkf,lk->snrlf/dot_general | solution.py:66
  1646.9 18.6 copy.44
  1665.5 55.1 %convert_bitcast_fusion = bf16[80,2,640,128]{2,3,1,0:T(8,128)(2,1)} fusion(bf16[80,640,640]{2,1,0:T(8,128)(2,1)} %param.7, bf16[80,640,2,128]{1,0,3,2:T(8,128)(2,1)} %bitcast.100), kind=kOutput, calls=%fused_computation.19 | convolution fusion | flops 16790323200 | bytes 117964800 | tf_op jit(solution)/shard_map/sna,snrc->srac/dot_general | solution.py:45
  1720.6 6.9 fusion.29
  1727.5 8.3 fusion.28
  1735.8 6.4 fusion.27
  1742.2 8.2 fusion.26
  1750.4 8.2 fusion.25
  1758.6 6.4 fusion.24
  1765.0 8.1 fusion.23
  1773.2 6.5 fusion.22
  1779.7 43.1 %copy.46 = bf16[8,80,2,80,128]{4,3,2,1,0:T(8,128)(2,1)} copy(bf16[8,80,2,80,128]{3,4,2,1,0:T(8,128)(2,1)} %fusion.22) | data formatting | bytes 52428800 | tf_op jit(solution)/shard_map/stack | solution.py:72
  1822.8 0.0 copy-start.4
  1822.8 575.5 %all_to_all.23 = bf16[8,80,2,80,128]{4,3,2,1,0:T(8,128)(2,1)} all-to-all(bf16[8,80,2,80,128]{4,3,2,1,0:T(8,128)(2,1)} %copy.46), channel_id=1, replica_groups=mesh['lat'=8,'lev'=4] {'lat'}, dimensions={0} | all-to-all | bytes 52428800 | tf_op jit(solution)/shard_map/all_to_all | solution.py:72
  2398.3 0.0 copy-done.4
  2398.3 18.0 bitcast_multiply_fusion
  2416.2 0.0 copy-start.3
  2416.2 42.8 %copy.47 = bf16[80,128,640,2]{2,0,3,1:T(8,128)(2,1)} copy(bf16[80,128,640,2]{1,0,3,2:T(8,128)(2,1)} %bitcast.96) | data formatting | bytes 52428800 | tf_op jit(solution)/shard_map/mrac,mrx->acx/dot_general | solution.py:77
  2459.1 0.0 copy-done.2
  2459.1 0.0 copy-done.3
  2459.1 0.0 copy-start.1
  2459.1 71.0 %bitcast_convert_fusion = bf16[80,32,4,1280]{3,1,2,0:T(8,128)(2,1)} fusion(bf16[80,32,4,640,2]{3,0,4,2,1:T(8,128)(2,1)} %bitcast.98, bf16[640,1,1280]{2,0,1:T(8,128)(2,1)S(1)} %copy-done.3, bf16[640,1,1280]{2,0,1:T(8,128)(2,1)S(1)} %copy-done.2), kind=kOutput, calls=%fused_computation.6 | convolution fusion | flops 33569177600 | bytes 55705600 | tf_op jit(solution)/shard_map/mrac,mrx->acx/dot_general | solution.py:77
  2530.1 29.9 %copy.49 = bf16[80,32,4,1280]{3,2,1,0:T(4,128)(2,1)} copy(bf16[80,32,4,1280]{3,1,2,0:T(8,128)(2,1)} %bitcast_convert_fusion) | data formatting | bytes 52428800 | tf_op jit(solution)/shard_map/convert_element_type | solution.py:80
  2560.0 0.0 copy-done.1
  (3 shorter events, 0.0 us)
Async XLA Ops:
  6.5 1575.4 %copy-start = (bf16[32,128]{1,0:T(8,128)(2,1)S(1)}, bf16[32,128]{1,0:T(8,128)(2,1)}, u32[]{:S(2)}) copy-start(bf16[32,128]{1,0:T(8,128)(2,1)} %param.8) | copy-start | bytes 24580
  166.7 574.0 %all-to-all-start = ((bf16[640,2,80,128]{3,2,1,0:T(8,128)(2,1)}), bf16[640,2,80,128]{3,2,1,0:T(8,128)(2,1)}, u32[]{:S(2)}, u32[]{:S(2)}) async-start(bf16[640,2,80,128]{3,2,1,0:T(8,128)(2,1)} %multiply_convert_fusion.1), calls=%async_computation | async-start | bytes 52428800 | tf_op jit(solution)/shard_map/all_to_all | solution.py:59
  174.0 1239.6 %all-gather.2.cloned.1.call-start = ((), (), s32[]{:S(2)}) async-start(), calls=%async_computation.2 | async-start | bytes 131072000 | tf_op jit(solution)/shard_map/all_gather | solution.py:63
  805.4 0.7 copy-start.5
  1822.8 575.5 %copy-start.4 = (bf16[640,80]{1,0:T(8,128)(2,1)S(1)}, bf16[640,80]{1,0:T(8,128)(2,1)}, u32[]{:S(2)}) copy-start(bf16[640,80]{1,0:T(8,128)(2,1)} %get-tuple-element.7) | copy-start | bytes 307204
  2416.2 42.8 %copy-start.2 = (bf16[640,1,1280]{2,0,1:T(8,128)(2,1)S(1)}, bf16[640,1,1280]{2,0,1:T(8,128)(2,1)}, u32[]{:S(2)}) copy-start(bf16[640,1,1280]{2,0,1:T(8,128)(2,1)} %get-tuple-element.5) | copy-start | bytes 4915204
  2416.2 42.9 %copy-start.3 = (bf16[640,1,1280]{2,0,1:T(8,128)(2,1)S(1)}, bf16[640,1,1280]{2,0,1:T(8,128)(2,1)}, u32[]{:S(2)}) copy-start(bf16[640,1,1280]{2,0,1:T(8,128)(2,1)} %get-tuple-element.6) | copy-start | bytes 4915204
  2459.1 100.9 %copy-start.1 = (bf16[32,128]{1,0:T(8,128)(2,1)S(1)}, bf16[32,128]{1,0:T(8,128)(2,1)}, u32[]{:S(2)}) copy-start(bf16[32,128]{1,0:T(8,128)(2,1)} %param.8) | copy-start | bytes 24580
Sparse Core Ops, SparseCore 0:
  805.6 607.9 all-gather.1
